TPU v7x, 32 devices: a whole 2x2x4 slice. The times are simulated.
32 devices in a mesh: groups: 2 (over y), seq: 4 (over z), head: 2 (over x), sub: 2 (over core).
Axes of the slice: x: 2, y: 2, z: 4, core: 2. Of those that a mesh axis runs over, the one named last changes fastest.
Arguments:
- queries: bfloat16 [8192, 4096], P(('groups', 'seq'), 'head'), parts along dimension 0, may hold values from -48 to 48
- keys: bfloat16 [8192, 1024], P(('groups', 'seq', 'sub'), 'head'), parts along dimension 0, may hold values from -18 to 18
- values: bfloat16 [8192, 1024], P(('groups', 'seq', 'sub'), 'head'), parts along dimension 0, may hold values from -6 to 6
- doc_lengths: int32 [16], P('groups'), parts along dimension 0, may hold values from 1 to 2048, 4096 in all
Outputs:
- attended: bfloat16 [8192, 4096], P(('groups', 'seq'), 'head'), parts along dimension 0
There are 2 independent parts, one for each index of `groups`. A program takes and returns all parts, laid end to end along the dimension named above; each array names one. Nothing has to cross between parts.
Inputs may be any that keep to these rules, and one draw needn't show every extreme that they name: `doc_lengths`: the 8 lengths sum to 4096; one of them is exactly 2048.
All inputs are finite; a program needn't handle non-finite values.
Results may differ from a plain program's by a relative error of at most 0.0036.
Values may be sent and summed in bfloat16 or wider, within the bound.
A program may use at most 192 MiB of HBM per device.

v0:
```python
import math

import jax
import jax.numpy as jnp
from jax import lax
from jax.sharding import PartitionSpec as P

DH = 128
SPAN = 2


lowest_start = -1e30


def shifted(value, axis, steps):
    count = lax.axis_size(axis)
    leading, last = (max(0, -steps), min(count, count - steps))
    return lax.ppermute(value, axis, [(source, source + steps) for source in range(leading, last)])


def document_of(positions, starts):
    return jnp.sum((starts[None, :] <= positions[:, None]).astype(jnp.int32), axis=1) - 1


def update_block(carried, query_block, key_block, value_block, allowed, scaling):
    running_max, running_sum, weighted = carried
    kv_heads = weighted.shape[1]
    keys_shaped = key_block.reshape(key_block.shape[0], kv_heads, DH)
    values_shaped = value_block.reshape(value_block.shape[0], kv_heads, DH)
    scores = (
        jnp.einsum("qagd,kad->qagk", query_block, keys_shaped, preferred_element_type=jnp.float32)
        * scaling
    )
    scores = jnp.where(allowed[:, None, None, :], scores, -jnp.inf)
    new_max = jnp.maximum(running_max, jnp.max(scores, axis=-1))
    factor = jnp.exp(running_max - new_max)
    weights = jnp.exp(scores - new_max[..., None])
    running_sum = running_sum * factor + jnp.sum(weights, axis=-1)
    product = jnp.einsum(
        "qagk,kad->qagd",
        weights.astype(jnp.bfloat16),
        values_shaped,
        preferred_element_type=jnp.float32,
    )
    weighted = weighted * factor[..., None] + product
    return (new_max, running_sum, weighted)


def attend(query_rows, query_start, blocks, starts):
    row_count = query_rows.shape[0]
    heads_total = query_rows.shape[1] // DH
    kv_heads = blocks[0][0].shape[1] // DH
    per_group = heads_total // kv_heads
    block_rows = min(512, row_count)
    scaling = 1.0 / math.sqrt(DH)
    query_block = query_rows
    query_block = query_block.reshape(block_rows, kv_heads, per_group, DH)
    query_pos = query_start + 0 + jnp.arange(block_rows, dtype=jnp.int32)
    query_doc = document_of(query_pos, starts)
    carried = (
        jnp.full((block_rows, kv_heads, per_group), lowest_start, jnp.float32),
        jnp.zeros((block_rows, kv_heads, per_group), jnp.float32),
        jnp.zeros((block_rows, kv_heads, per_group, DH), jnp.float32),
    )
    for key_block, value_block, key_start in blocks:
        key_pos = key_start + jnp.arange(key_block.shape[0], dtype=jnp.int32)
        key_doc = document_of(key_pos, starts)
        allowed = (key_pos[None, :] <= query_pos[:, None]) & (
            key_doc[None, :] == query_doc[:, None]
        )
        carried = update_block(carried, query_block, key_block, value_block, allowed, scaling)
    results = [carried]
    return tuple(
        (jnp.concatenate([piece[member] for piece in results], axis=0) for member in range(3))
    )


def shards(queries, keys, values, doc_lengths):
    row_count = queries.shape[0]
    half_rows = keys.shape[0]
    seq_place = lax.axis_index("seq")
    sub_place = lax.axis_index("sub")
    starts = jnp.cumsum(doc_lengths) - doc_lengths
    own_start = seq_place * row_count + sub_place * half_rows
    blocks = [(keys, values, own_start)]
    for offset in range(1, SPAN + 1):
        moved_keys, moved_values = shifted((keys, values), "seq", offset)
        blocks.append((moved_keys, moved_values, own_start - offset * row_count))
    stacked_keys = jnp.stack([triple[0] for triple in blocks])
    stacked_values = jnp.stack([triple[1] for triple in blocks])
    whole_keys, whole_values = (
        lax.all_gather(stacked_keys, "sub", axis=1, tiled=True),
        lax.all_gather(stacked_values, "sub", axis=1, tiled=True),
    )
    wide_blocks = [
        (whole_keys[number], whole_values[number], seq_place * row_count - number * row_count)
        for number in range(SPAN + 1)
    ]
    own_queries = lax.dynamic_slice_in_dim(queries, sub_place * half_rows, half_rows, 0)
    highest, denominator, weighted = attend(own_queries, own_start, wide_blocks, starts)
    partial_rows = (weighted / denominator[..., None]).reshape(half_rows, -1).astype(jnp.bfloat16)
    return lax.all_gather(partial_rows, "sub", axis=0, tiled=True)


def solution(mesh):
    placed = (
        P(("groups", "seq"), "head"),
        P(("groups", "seq", "sub"), "head"),
        P(("groups", "seq", "sub"), "head"),
        P("groups"),
    )
    return jax.shard_map(
        shards, mesh=mesh, in_specs=placed, out_specs=P(("groups", "seq"), "head"), check_vma=False
    )
```

profile of v0, /device:TPU:17, one launch (start us, length us, event | category | flops | bytes accessed | tf_op | source)
XLA Modules:
  0.0 271.6 jit_solution(7642718932861351261)
XLA Ops:
  6.5 0.0 copy-start.3
  6.5 0.0 all-gather.6.cloned.1.call-start
  6.5 1.4 collective-permute-start.3
  8.0 3.2 %collective-permute-start.2 = (bf16[512,512]{1,0:T(8,128)(2,1)}, bf16[512,512]{1,0:T(8,128)(2,1)S(1)}, u32[]{:S(2)}, u32[]{:S(2)}) collective-permute-start(bf16[512,512]{1,0:T(8,128)(2,1)} %param.6), channel_id=1, source_target_pairs={{0,4},{4,8},{8,12},{1,5},{5,9},{9,13},{2,6},{6,10},{10,14},{3,7},{... | collective-permute-start | bytes 1572872 | tf_op jit(solution)/shard_map/ppermute | solution.py:18
  11.2 11.3 %collective-permute-done.3 = bf16[512,512]{1,0:T(8,128)(2,1)S(1)} collective-permute-done((bf16[512,512]{1,0:T(8,128)(2,1)}, bf16[512,512]{1,0:T(8,128)(2,1)S(1)}, u32[]{:S(2)}, u32[]{:S(2)}) %collective-permute-start.3) | collective-permute-done | bytes 524320 | tf_op jit(solution)/shard_map/ppermute | solution.py:18
  22.5 23.5 %collective-permute-done.2 = bf16[512,512]{1,0:T(8,128)(2,1)S(1)} collective-permute-done((bf16[512,512]{1,0:T(8,128)(2,1)}, bf16[512,512]{1,0:T(8,128)(2,1)S(1)}, u32[]{:S(2)}, u32[]{:S(2)}) %collective-permute-start.2) | collective-permute-done | bytes 524320 | tf_op jit(solution)/shard_map/ppermute | solution.py:18
  46.0 2.4 pad_maximum_fusion.1
  48.5 0.0 all-gather.6.cloned.1.call-update
  48.5 0.0 all-gather.4.cloned.1.call-start
  48.5 1.3 copy.29
  49.8 1.3 collective-permute-start.1
  51.1 1.9 collective-permute-start
  53.0 12.6 %collective-permute-done.1 = bf16[512,512]{0,1:T(8,128)(2,1)S(1)} collective-permute-done((bf16[512,512]{0,1:T(8,128)(2,1)S(1)}, bf16[512,512]{0,1:T(8,128)(2,1)S(1)}, u32[]{:S(2)}, u32[]{:S(2)}) %collective-permute-start.1) | collective-permute-done | bytes 524320 | tf_op jit(solution)/shard_map/ppermute | solution.py:18
  65.6 19.1 %collective-permute-done = bf16[512,512]{0,1:T(8,128)(2,1)S(1)} collective-permute-done((bf16[512,512]{0,1:T(8,128)(2,1)S(1)}, bf16[512,512]{0,1:T(8,128)(2,1)S(1)}, u32[]{:S(2)}, u32[]{:S(2)}) %collective-permute-start) | collective-permute-done | bytes 524320 | tf_op jit(solution)/shard_map/ppermute | solution.py:18
  84.7 1.3 pad_maximum_fusion
  86.0 0.0 all-gather.4.cloned.1.call-update
  86.1 0.0 all-gather.8.cloned.1.call-start
  86.1 0.8 reduce-window.9
  87.0 3.2 %constant_dynamic-slice_fusion = bf16[512,2048]{1,0:T(8,128)(2,1)} fusion(bf16[1024,2048]{1,0:T(8,128)(2,1)} %param.4, s32[]{:T(128)S(6)} %select_n.13), kind=kLoop, calls=%fused_computation.51 | loop fusion | bytes 4194308 | tf_op jit(solution)/shard_map/dynamic_slice | solution.py:99
  90.1 2.9 %copy.64 = bf16[512,2048]{0,1:T(8,128)(2,1)S(1)} copy(bf16[512,2048]{1,0:T(8,128)(2,1)} %constant_dynamic-slice_fusion) | data formatting | bytes 4194304
  93.0 0.0 copy-done.3
  93.1 0.1 convert_reduce_fusion.3
  93.1 0.1 convert_reduce_fusion
  93.3 2.4 compare_and_fusion.2
  95.7 0.0 all-gather.6.cloned.1.call-done
  95.7 4.1 %fusion.33 = (bf16[1,1024,512]{2,1,0:T(8,128)(2,1)}, bf16[1,1024,512]{2,1,0:T(8,128)(2,1)}, bf16[1,1024,512]{2,1,0:T(8,128)(2,1)}) fusion(bf16[3,1024,512]{2,1,0:T(8,128)(2,1)} %all-gather.6.cloned.1.call-done), kind=kLoop, calls=%fused_computation.60 | loop fusion | bytes 6291456 | tf_op jit(solution)/shard_map/slice | solution.py:96
  99.8 2.3 copy.35
  102.1 2.3 copy.43
  104.3 2.3 copy.39
  106.6 0.0 all-gather.4.cloned.1.call-done
  106.6 2.2 fusion.34
  108.8 13.5 %fusion.6 = (f32[512,4,4]{0,2,1:T(4,128)S(1)}, f32[4,1024,512,4]{2,1,3,0:T(8,128)}) fusion(pred[512,1024]{0,1:T(8,128)(4,1)S(1)} %get-tuple-element.21, bf16[1024,4,128,1]{0,2,3,1:T(8,128)(2,1)S(1)} %bitcast.102, bf16[512,4,4,128]{0,3,2,1:T(8,128)(2,1)S(1)} %bitcast.97), kind=kOutput, calls=%fused_computation.12 | convolution fusion | flops 2172641280 | bytes 37257216 | tf_op jit(solution)/shard_map/qagd,kad->qagk/dot_general | solution.py:31
  122.2 0.0 copy-start
  122.2 13.5 %fusion.7 = (f32[512,4,4]{0,2,1:T(4,128)S(1)}, f32[4,1024,512,4]{2,1,3,0:T(8,128)}) fusion(pred[512,1024]{0,1:T(8,128)(4,1)S(1)} %get-tuple-element.22, bf16[1024,4,128,1]{0,2,3,1:T(8,128)(2,1)S(1)} %bitcast.101, bf16[512,4,4,128]{0,3,2,1:T(8,128)(2,1)S(1)} %bitcast.98), kind=kOutput, calls=%fused_computation.13 | convolution fusion | flops 2172641280 | bytes 37257216 | tf_op jit(solution)/shard_map/qagd,kad->qagk/dot_general | solution.py:31
  135.7 0.0 copy-done
  135.7 13.4 %fusion.8 = (f32[512,4,4]{0,2,1:T(4,128)S(1)}, f32[4,1024,512,4]{2,1,3,0:T(8,128)}) fusion(pred[512,1024]{0,1:T(8,128)(4,1)S(1)} %copy-done, bf16[1024,4,128,1]{0,2,3,1:T(8,128)(2,1)S(1)} %bitcast.100, bf16[512,4,4,128]{0,3,2,1:T(8,128)(2,1)S(1)} %bitcast.99), kind=kOutput, calls=%fused_computation.14 | convolution fusion | flops 2172641280 | bytes 37257216 | tf_op jit(solution)/shard_map/qagd,kad->qagk/dot_general | solution.py:31
  149.2 0.0 copy-start.2
  149.2 14.5 %fusion.4 = f32[512,4,4]{0,2,1:T(4,128)S(1)} fusion(f32[4,1024,512,4]{2,1,3,0:T(8,128)} %get-tuple-element.25, f32[512,4,4]{0,2,1:T(4,128)S(1)} %get-tuple-element.11, pred[512,1024]{0,1:T(8,128)(4,1)S(1)} %copy-done), kind=kLoop, calls=%fused_computation.10 | loop fusion | flops 33546240 | bytes 34144256 | tf_op jit(solution)/shard_map/reduce_sum | solution.py:38
  163.7 0.0 copy-done.2
  163.7 16.2 %fusion.9 = f32[4,128,512,4]{2,1,3,0:T(8,128)} fusion(bf16[1024,4,128,1]{0,2,3,1:T(8,128)(2,1)S(1)} %bitcast.107, f32[4,1024,512,4]{2,1,3,0:T(8,128)} %get-tuple-element.25, f32[512,4,4]{0,2,1:T(4,128)S(1)} %get-tuple-element.11, pred[512,1024]{0,1:T(8,128)(4,1)S(1)} %copy-done), kind=kOutput, calls=%fused_computation.15 | convolution fusion | flops 2181038080 | bytes 39354368 | tf_op jit(solution)/shard_map/qagk,kad->qagd/dot_general | solution.py:39
  179.9 0.0 copy-start.1
  179.9 14.4 %fusion.2 = f32[512,4,4]{0,2,1:T(4,128)S(1)} fusion(f32[4,1024,512,4]{2,1,3,0:T(8,128)} %get-tuple-element.27, f32[512,4,4]{0,2,1:T(4,128)S(1)} %get-tuple-element.12, pred[512,1024]{0,1:T(8,128)(4,1)S(1)} %get-tuple-element.22), kind=kLoop, calls=%fused_computation.8 | loop fusion | flops 33546240 | bytes 34144256 | tf_op jit(solution)/shard_map/reduce_sum | solution.py:38
  194.3 0.0 copy-done.1
  194.3 16.1 %fusion.11 = f32[4,128,512,4]{2,1,3,0:T(8,128)} fusion(bf16[1024,4,128,1]{0,2,3,1:T(8,128)(2,1)S(1)} %bitcast.106, f32[4,1024,512,4]{2,1,3,0:T(8,128)} %get-tuple-element.27, f32[512,4,4]{0,2,1:T(4,128)S(1)} %get-tuple-element.12, pred[512,1024]{0,1:T(8,128)(4,1)S(1)} %get-tuple-element.22), kind=kOutput, calls=%fused_computation.16 | convolution fusion | flops 2181038080 | bytes 39354368 | tf_op jit(solution)/shard_map/qagk,kad->qagd/dot_general | solution.py:39
  210.4 14.3 %fusion = f32[512,4,4]{0,2,1:T(4,128)S(1)} fusion(f32[4,1024,512,4]{2,1,3,0:T(8,128)} %get-tuple-element.29, f32[512,4,4]{0,2,1:T(4,128)S(1)} %get-tuple-element.20, pred[512,1024]{0,1:T(8,128)(4,1)S(1)} %get-tuple-element.21), kind=kLoop, calls=%fused_computation.6 | loop fusion | flops 33546240 | bytes 34144256 | tf_op jit(solution)/shard_map/reduce_sum | solution.py:38
  224.8 0.1 multiply_add_fusion
  224.8 18.0 %fusion.19 = bf16[512,4,4,128]{0,3,2,1:T(8,128)(2,1)S(1)} fusion(f32[4,128,512,4]{2,1,3,0:T(8,128)} %fusion.9, f32[4,128,512,4]{2,1,3,0:T(8,128)} %fusion.11, bf16[1024,4,128,1]{0,2,3,1:T(8,128)(2,1)} %bitcast.105, f32[4,1024,512,4]{2,1,3,0:T(8,128)} %get-tuple-element.29, f32[512,4,4]{0,2,1:T(4,128)S(1)} %get-tuple-element.20, ...), kind=kOutput, calls=%fused_computation.23 | convolution fusion | flops 2188378112 | bytes 45776896 | tf_op jit(solution)/shard_map/qagk,kad->qagd/dot_general | solution.py:39
  242.9 2.4 copy.45
  245.3 0.0 all-gather.8.cloned.1.call-update
  245.3 15.0 %all-gather.8.cloned.1.call-done = bf16[1024,2048]{1,0:T(8,128)(2,1)} async-done(((bf16[512,2048]{1,0:T(8,128)(2,1)}), bf16[1024,2048]{1,0:T(8,128)(2,1)}) %all-gather.8.cloned.1.call-update) | async-done | bytes 4194320 | tf_op jit(solution)/shard_map/all_gather | solution.py:102
  260.3 4.8 %copy.66 = bf16[1024,2048]{1,0:T(8,128)(2,1)} copy(bf16[1024,2048]{1,0:T(8,128)(2,1)} %all-gather.8.cloned.1.call-done) | data formatting | bytes 8388608
  (9 shorter events, 0.1 us)
Async XLA Ops:
  6.5 86.5 %copy-start.3 = (s32[8]{0:T(128)S(1)}, s32[8]{0:T(128)}, u32[]{:S(2)}) copy-start(s32[8]{0:T(128)} %param.7) | copy-start | bytes 100
  6.5 89.2 %all-gather.6.cloned.1.call-start = ((), (), s32[]{:S(2)}) async-start(), calls=%async_computation.1 | async-start | bytes 4718592 | tf_op jit(solution)/shard_map/all_gather | solution.py:93
  6.5 16.0 %collective-permute-start.3 = (bf16[512,512]{1,0:T(8,128)(2,1)}, bf16[512,512]{1,0:T(8,128)(2,1)S(1)}, u32[]{:S(2)}, u32[]{:S(2)}) collective-permute-start(bf16[512,512]{1,0:T(8,128)(2,1)} %param.6), channel_id=1, source_target_pairs={{0,8},{4,12},{1,9},{5,13},{2,10},{6,14},{3,11},{7,15},{16,24},{20,... | collective-permute-start | bytes 1572872 | tf_op jit(solution)/shard_map/ppermute | solution.py:18
  8.0 38.1 %collective-permute-start.2 = (bf16[512,512]{1,0:T(8,128)(2,1)}, bf16[512,512]{1,0:T(8,128)(2,1)S(1)}, u32[]{:S(2)}, u32[]{:S(2)}) collective-permute-start(bf16[512,512]{1,0:T(8,128)(2,1)} %param.6), channel_id=1, source_target_pairs={{0,4},{4,8},{8,12},{1,5},{5,9},{9,13},{2,6},{6,10},{10,14},{3,7},{... | collective-permute-start | bytes 1572872 | tf_op jit(solution)/shard_map/ppermute | solution.py:18
  48.5 58.1 %all-gather.4.cloned.1.call-start = ((), (), s32[]{:S(2)}) async-start(), calls=%async_computation | async-start | bytes 4718592 | tf_op jit(solution)/shard_map/all_gather | solution.py:92
  49.8 15.8 %collective-permute-start.1 = (bf16[512,512]{0,1:T(8,128)(2,1)S(1)}, bf16[512,512]{0,1:T(8,128)(2,1)S(1)}, u32[]{:S(2)}, u32[]{:S(2)}) collective-permute-start(bf16[512,512]{0,1:T(8,128)(2,1)S(1)} %copy.29), channel_id=1, source_target_pairs={{0,8},{4,12},{1,9},{5,13},{2,10},{6,14},{3,11},{7,15},{16,24},{20,... | collective-permute-start | bytes 1572872 | tf_op jit(solution)/shard_map/ppermute | solution.py:18
  51.1 33.6 %collective-permute-start = (bf16[512,512]{0,1:T(8,128)(2,1)S(1)}, bf16[512,512]{0,1:T(8,128)(2,1)S(1)}, u32[]{:S(2)}, u32[]{:S(2)}) collective-permute-start(bf16[512,512]{0,1:T(8,128)(2,1)S(1)} %copy.29), channel_id=1, source_target_pairs={{0,4},{4,8},{8,12},{1,5},{5,9},{9,13},{2,6},{6,10},{10,14},{3,7},{... | collective-permute-start | bytes 1572872 | tf_op jit(solution)/shard_map/ppermute | solution.py:18
  86.1 174.2 %all-gather.8.cloned.1.call-start = ((), (), s32[]{:S(2)}) async-start(), calls=%async_computation.2 | async-start | bytes 6291456 | tf_op jit(solution)/shard_map/all_gather | solution.py:102
  122.2 13.5 %copy-start = (pred[512,1024]{0,1:T(8,128)(4,1)S(1)}, pred[512,1024]{0,1:T(8,128)(4,1)}, u32[]{:S(2)}) copy-start(pred[512,1024]{0,1:T(8,128)(4,1)} %get-tuple-element.23) | copy-start | bytes 1572868
  149.2 14.5 %copy-start.2 = (bf16[1,1024,512]{1,2,0:T(8,128)(2,1)S(1)}, bf16[1,1024,512]{1,2,0:T(8,128)(2,1)}, u32[]{:S(2)}) copy-start(bf16[1,1024,512]{1,2,0:T(8,128)(2,1)} %copy.43) | copy-start | bytes 3145732
  179.9 14.4 %copy-start.1 = (bf16[1,1024,512]{1,2,0:T(8,128)(2,1)S(1)}, bf16[1,1024,512]{1,2,0:T(8,128)(2,1)}, u32[]{:S(2)}) copy-start(bf16[1,1024,512]{1,2,0:T(8,128)(2,1)} %copy.39) | copy-start | bytes 3145732
Sparse Core Ops, SparseCore 0:
  48.6 12.7 all-gather.5
  86.2 13.3 all-gather.3
  245.4 14.8 all-gather.7
where the time goes:
time: 273 us; the launch traced here: 272 us
  matrix products  90.7 us (33%)
  waiting for transfers between devices  81.6 us (30%)
  other arithmetic  50.6 us (19%)
  local copies, waits for them, and re-layouts  27.5 us (10%)
  between operations  13.3 us (5%)
  starting transfers between devices  7.91 us (3%)
    ppermute x4, waiting for transfers between devices, shifted(): lax.ppermute(value, axis, [(source, source + steps) for source in range(l...  66.5 us
    dot_general x3, matrix products, update_block(): jnp.einsum('qagk,kad->qagd', weights.astype(jnp.bfloat16), values_shaped,...  50.3 us
    reduce_sum x3, other arithmetic, update_block(): running_sum = running_sum * factor + jnp.sum(weights, axis=-1)  43.3 us
    dot_general x3, matrix products, update_block(): jnp.einsum('qagd,kad->qagk', query_block, keys_shaped, preferred_element_...  40.4 us
    all_gather x1, waiting for transfers between devices, shards(): return lax.all_gather(partial_rows, 'sub', axis=0, tiled=True)  15 us
    slice x4, local copies, waits for them, and re-layouts, shards(): whole_values[number]  10.9 us
    unnamed x11, local copies, waits for them, and re-layouts  8.92 us
    ppermute x4, starting transfers between devices, shifted(): lax.ppermute(value, axis, [(source, source + steps) for source in range(l...  7.83 us
  transfers between devices with their start and end apart: 7, of which 5 were waited for; matrix products, arithmetic and copies ran while one was open for 8% of the time, Pallas kernels for 0%

commit v1 on v0

v1 whole, which is shorter than its diff:
```python
import functools
import math

import jax
import jax.numpy as jnp
from jax import lax
from jax.experimental import pallas as pl
from jax.experimental.pallas import tpu as pltpu
from jax.sharding import PartitionSpec as P

DH = 128
SPAN = 2
LANES = 128
BLOCKED = -1048576.0
LEAST = -1e30
MESH = pl.DeviceIdType.MESH
SCALE = math.log2(math.e) / math.sqrt(DH)


def attention_kernel(
    sizes, lengths, q_hbm, k_hbm, v_hbm, out,
    q_vm, kbuf, vbuf, qx, kx, top, acc, obuf,
    load_sem, swap_sem, hop_sem, recv_sem, out_send, out_recv, out_local,
):
    n_seq, rows, half, kv_cols, q_cols, split_kv, n_docs, rows_q = sizes
    seq, sub = lax.axis_index("seq"), lax.axis_index("sub")
    other = 1 - sub
    heads, kv_heads = q_cols // DH, kv_cols // DH
    group = heads // kv_heads
    has_prev, has_next = seq > 0, seq < n_seq - 1

    my_cols = pl.ds(pl.multiple_of(sub * kv_cols, LANES), kv_cols) if split_kv else pl.ds(0, kv_cols)
    its_cols = pl.ds(pl.multiple_of(other * kv_cols, LANES), kv_cols) if split_kv else pl.ds(0, kv_cols)
    my_q = pl.ds(pl.multiple_of(sub * q_cols, LANES), q_cols)

    loads = [
        pltpu.make_async_copy(k_hbm.at[:, my_cols], kbuf.at[0, sub], load_sem.at[0]),
        pltpu.make_async_copy(v_hbm.at[:, my_cols], vbuf.at[0, sub], load_sem.at[1]),
        pltpu.make_async_copy(q_hbm.at[:, my_q], q_vm, load_sem.at[2]),
    ]
    for load in loads:
        load.start()

    barrier = pltpu.get_barrier_semaphore()
    pl.semaphore_signal(barrier, inc=1, device_id={"sub": other}, device_id_type=MESH)

    @pl.when(has_prev)
    def _():
        pl.semaphore_signal(barrier, inc=1, device_id={"seq": seq - 1}, device_id_type=MESH)

    @pl.when(has_next)
    def _():
        pl.semaphore_signal(barrier, inc=1, device_id={"seq": seq + 1}, device_id_type=MESH)

    peers = 1 + jnp.minimum(seq, 1) + jnp.minimum(n_seq - 1 - seq, 1)
    pl.semaphore_wait(barrier, peers)

    def remote(src, dst, send, recv, where):
        return pltpu.make_async_remote_copy(
            src_ref=src, dst_ref=dst, send_sem=send, recv_sem=recv, device_id=where, device_id_type=MESH
        )

    swaps = [
        remote(hbm.at[:, its_cols], buf.at[0, sub], swap_sem.at[kind], recv_sem.at[0, sub, kind], {"sub": other})
        for kind, (hbm, buf) in enumerate(((k_hbm, kbuf), (v_hbm, vbuf)))
    ]
    for swap in swaps:
        swap.start()

    def hops(slot, part):
        return [
            remote(
                buf.at[slot, part], buf.at[slot + 1, part],
                hop_sem.at[slot, part, kind], recv_sem.at[slot + 1, part, kind], {"seq": seq + 1},
            )
            for kind, buf in enumerate((kbuf, vbuf))
        ]

    def wait_arrival(slot, part):
        for kind, buf in enumerate((kbuf, vbuf)):
            pltpu.make_async_copy(buf.at[slot, part], buf.at[slot, part], recv_sem.at[slot, part, kind]).wait()

    def start_hops(slot, part):
        @pl.when(has_next)
        def _():
            for hop in hops(slot, part):
                hop.start()

    loads[0].wait()
    loads[1].wait()
    start_hops(0, sub)

    lane = lax.broadcasted_iota(jnp.int32, (1, LANES), 1)
    lows = jnp.full((1, LANES), 2**30, jnp.int32)
    highs = jnp.full((1, LANES), 2**30, jnp.int32)
    begin = jnp.int32(0)
    for d in range(n_docs):
        end = begin + lengths[d]
        lows = jnp.where(lane == d, begin, lows)
        highs = jnp.where(lane == d, end, highs)
        begin = end
    block = 256

    def fill(i, _):
        row0 = pl.multiple_of(i * block, block)
        base = lax.broadcasted_iota(jnp.int32, (block, LANES), 0) + row0 + seq * rows
        for slot in range(SPAN + 1):
            place = base - slot * rows
            inside = (place >= lows) & (place < highs)
            kx[slot, pl.ds(row0, block), :] = jnp.where(inside, 1.0, 0.0).astype(jnp.bfloat16)
            if slot == 0:
                qx[pl.ds(row0, block), :] = jnp.where(inside, 0.0, BLOCKED).astype(jnp.bfloat16)
        return 0

    lax.fori_loop(0, rows // block, fill, 0)

    wait_arrival(0, other)
    start_hops(0, other)
    loads[2].wait()

    ones = jnp.ones((half, DH), jnp.bfloat16)

    def wide(x, times):
        return jnp.concatenate([x] * times, axis=1)

    def update(slot, part, row0, kv, first, offset):
        keys = jnp.concatenate(
            [kbuf[slot, part, :, pl.ds(pl.multiple_of(kv * DH, DH), DH)],
             kx[slot, pl.ds(pl.multiple_of(part * half, half), half), :]], axis=1)
        vals = jnp.concatenate([vbuf[slot, part, :, pl.ds(pl.multiple_of(kv * DH, DH), DH)], ones], axis=1)
        q_rows = pl.ds(row0, rows_q)
        if offset is not None:
            row_at = lax.broadcasted_iota(jnp.int32, (rows_q, half), 0) + offset
            causal = lax.broadcasted_iota(jnp.int32, (rows_q, half), 1) <= row_at
        for g in range(group):
            h = kv * group + g
            query = jnp.concatenate(
                [q_vm[q_rows, pl.ds(pl.multiple_of(h * DH, DH), DH)], qx[q_rows, :]], axis=1)
            scores = lax.dot_general(
                query, keys, (((1,), (1,)), ((), ())), preferred_element_type=jnp.float32)
            if offset is not None:
                scores = jnp.where(causal, scores, LEAST)
            peak = jnp.max(scores, axis=1, keepdims=True)
            if first:
                new_top = jnp.broadcast_to(peak, (rows_q, LANES))
            else:
                old_top = top[h, q_rows, :]
                new_top = jnp.maximum(old_top, peak)
            weights = jnp.exp2((scores - wide(new_top, half // LANES)) * SCALE).astype(jnp.bfloat16)
            product = jnp.dot(weights, vals, preferred_element_type=jnp.float32)
            if first:
                acc[h, q_rows, :] = product
            else:
                factor = jnp.exp2((old_top - new_top) * SCALE)
                acc[h, q_rows, :] = acc[h, q_rows, :] * wide(factor, 2) + product
            top[h, q_rows, :] = new_top

    per_half = half // rows_q

    def sweep(slot, part, start, count, first, diagonal):
        def body(i, _):
            block_at, kv = i // kv_heads, i % kv_heads
            row0 = pl.multiple_of(start + block_at * rows_q, rows_q)
            update(slot, part, row0, kv, first, block_at * rows_q if diagonal else None)
            return 0

        lax.fori_loop(0, count * kv_heads, body, 0)

    sweep(0, 0, 0, per_half, True, True)
    sweep(0, 1, half, per_half, True, True)
    sweep(0, 0, half, per_half, False, False)

    for slot in range(1, SPAN + 1):
        @pl.when(seq >= slot)
        def _():
            for part in (sub, other):
                wait_arrival(slot, part)
                if slot < SPAN:
                    start_hops(slot, part)
                sweep(slot, part, 0, rows // rows_q, False, False)

    def sends(h):
        columns = pl.ds(pl.multiple_of(sub * q_cols + h * DH, DH), DH)
        return (
            remote(obuf.at[h], out.at[:, columns], out_send.at[h], out_recv.at[h], {"sub": other}),
            pltpu.make_async_copy(obuf.at[h], out.at[:, columns], out_local.at[h]),
        )

    for h in range(heads):
        obuf[h] = (acc[h, :, :DH] / acc[h, :, DH:]).astype(jnp.bfloat16)
        if h:
            for copy in sends(h - 1):
                copy.start()
    for h in range(heads):
        far, near = sends(h)
        if h == 0:
            near.wait()
            for copy in sends(heads - 1):
                copy.start()
        else:
            near.wait()
        far.wait()

    for swap in swaps:
        swap.wait_send()

    @pl.when(has_next)
    def _():
        for part in (sub, other):
            for hop in hops(0, part):
                hop.wait_send()

    for slot in range(1, SPAN):
        @pl.when((seq >= slot) & has_next)
        def _():
            for part in (sub, other):
                for hop in hops(slot, part):
                    hop.wait_send()


def shards(n_seq, queries, keys, values, doc_lengths):
    rows, q_total = queries.shape
    half, kv_total = keys.shape
    q_cols = q_total // 2
    split_kv = kv_total // DH >= 2
    kv_cols = kv_total // 2 if split_kv else kv_total
    heads = q_cols // DH
    sizes = (n_seq, rows, half, kv_cols, q_cols, split_kv, doc_lengths.shape[0], min(256, half))
    any_space = pl.BlockSpec(memory_space=pl.ANY)
    dma = pltpu.SemaphoreType.DMA
    return pl.pallas_call(
        functools.partial(attention_kernel, sizes),
        out_shape=jax.ShapeDtypeStruct((rows, q_total), jnp.bfloat16),
        in_specs=[pl.BlockSpec(memory_space=pltpu.SMEM)] + [any_space] * 3,
        out_specs=any_space,
        scratch_shapes=[
            pltpu.VMEM((rows, q_cols), jnp.bfloat16),
            pltpu.VMEM((SPAN + 1, 2, half, kv_cols), jnp.bfloat16),
            pltpu.VMEM((SPAN + 1, 2, half, kv_cols), jnp.bfloat16),
            pltpu.VMEM((rows, LANES), jnp.bfloat16),
            pltpu.VMEM((SPAN + 1, rows, LANES), jnp.bfloat16),
            pltpu.VMEM((heads, rows, LANES), jnp.float32),
            pltpu.VMEM((heads, rows, 2 * DH), jnp.float32),
            pltpu.VMEM((heads, rows, DH), jnp.bfloat16),
            dma((3,)),
            dma((2,)),
            dma((SPAN, 2, 2)),
            dma((SPAN + 1, 2, 2)),
            dma((heads,)),
            dma((heads,)),
            dma((heads,)),
        ],
        compiler_params=pltpu.CompilerParams(
            collective_id=0, has_side_effects=True, vmem_limit_bytes=60 * 1024 * 1024
        ),
    )(doc_lengths, queries, keys, values)


def solution(mesh):
    placed = (
        P(("groups", "seq"), "head"),
        P(("groups", "seq", "sub"), "head"),
        P(("groups", "seq", "sub"), "head"),
        P("groups"),
    )
    return jax.shard_map(
        functools.partial(shards, mesh.shape["seq"]),
        mesh=mesh, in_specs=placed, out_specs=P(("groups", "seq"), "head"), check_vma=False,
    )
```

time: 273 us -> 66.6 us (0.24)
  matrix products: 90.7 us -> 0 us
  waiting for transfers between devices: 81.6 us -> 0 us
  Pallas kernels: 0 us -> 61.6 us
  other arithmetic: 50.6 us -> 0 us
  local copies, waits for them, and re-layouts: 27.5 us -> 4.79 us
  between operations: 13.3 us -> 0.01 us
  starting transfers between devices: 7.91 us -> 0 us
    dot_general x6 -> x0, matrix products: 90.7 us -> none  [the longest x3 50.3 us: update_block(): jnp.einsum('qagk,kad->qagd', weights.astype(jnp.bfloat16), values_shaped,...]
    ppermute x4 -> x0, waiting for transfers between devices: 66.5 us -> none  [shifted(): lax.ppermute(value, axis, [(source, source + steps) for source in range(l...]
    pallas_call x0 -> x1, Pallas kernels: none -> 61.6 us  [shards(): pl.pallas_call(functools.partial(attention_kernel, sizes), out_shape=jax....]
    reduce_sum x5 -> x0, other arithmetic: 43.5 us -> none  [the longest x3 43.3 us: update_block(): running_sum = running_sum * factor + jnp.sum(weights, axis=-1)]
    all_gather x3 -> x0, waiting for transfers between devices: 15 us -> none  [the longest x1 15 us: shards(): return lax.all_gather(partial_rows, 'sub', axis=0, tiled=True)]
    slice x5 -> x0, local copies, waits for them, and re-layouts: 13.1 us -> none  [the longest x4 10.9 us: shards(): whole_values[number]]
    ppermute x4 -> x0, starting transfers between devices: 7.83 us -> none  [shifted(): lax.ppermute(value, axis, [(source, source + steps) for source in range(l...]
    another operation x3 -> x0, other arithmetic: 4.59 us -> none  [the longest x1 2.44 us: shards(): stacked_values = jnp.stack([triple[1] for triple in blocks])]
  transfers between devices with their start and end apart: 7 -> 0, of which waited for: 5 -> 0; matrix products, arithmetic and copies ran while one was open for 8% -> 0% of each run, Pallas kernels for 0% -> 0%
where the time goes in v1:
time: 66.6 us; the launch traced here: 66.4 us
  Pallas kernels  61.6 us (92%)
  local copies, waits for them, and re-layouts  4.79 us (7%)
    pallas_call x1, Pallas kernels, shards(): pl.pallas_call(functools.partial(attention_kernel, sizes), out_shape=jax....  61.6 us
    unnamed x1, local copies, waits for them, and re-layouts  4.79 us

profile of v1, /device:TPU:17, one launch (start us, length us, event | category | flops | bytes accessed | tf_op | source)
XLA Modules:
  0.0 66.4 jit_solution(9980823826139825912)
XLA Ops:
  0.0 61.6 %shard_map.46 = bf16[1024,2048]{1,0:T(8,128)(2,1)} custom-call(s32[8]{0:T(128)} %lengths.1, bf16[1024,2048]{1,0:T(8,128)(2,1)} %q_hbm.1, bf16[512,512]{1,0:T(8,128)(2,1)} %k_hbm.1, bf16[512,512]{1,0:T(8,128)(2,1)} %v_hbm.1), custom_call_target="tpu_custom_call" | custom-call | tf_op jit(solution)/shard_map/pallas_call | solution.py:231
  61.6 4.8 %copy.6 = bf16[1024,2048]{1,0:T(8,128)(2,1)} copy(bf16[1024,2048]{1,0:T(8,128)(2,1)} %shard_map.46) | data formatting | bytes 8388608

commit v2 on v1

v2 whole, which is shorter than its diff:
```python
import functools
import math

import jax
import jax.numpy as jnp
from jax import lax
from jax.experimental import pallas as pl
from jax.experimental.pallas import tpu as pltpu
from jax.sharding import PartitionSpec as P

DH = 128
SPAN = 2
LANES = 128
BLOCKED = -1048576.0
LEAST = -1e30
MESH = pl.DeviceIdType.MESH
SCALE = math.log2(math.e) / math.sqrt(DH)


def attention_kernel(
    sizes, lengths, q_hbm, k_hbm, v_hbm, out,
    q_vm, kbuf, vbuf, qx, kx, top, acc, obuf,
    load_sem, swap_sem, hop_sem, recv_sem, out_send, out_recv, out_local,
):
    n_seq, rows, half, kv_cols, q_cols, split_kv, n_docs, rows_q, pieces = sizes
    piece_rows = half // pieces
    seq, sub = lax.axis_index("seq"), lax.axis_index("sub")
    other = 1 - sub
    heads, kv_heads = q_cols // DH, kv_cols // DH
    group = heads // kv_heads
    has_prev, has_next = seq > 0, seq < n_seq - 1

    my_cols = pl.ds(pl.multiple_of(sub * kv_cols, LANES), kv_cols) if split_kv else pl.ds(0, kv_cols)
    its_cols = pl.ds(pl.multiple_of(other * kv_cols, LANES), kv_cols) if split_kv else pl.ds(0, kv_cols)
    my_q = pl.ds(pl.multiple_of(sub * q_cols, LANES), q_cols)

    loads = [
        pltpu.make_async_copy(k_hbm.at[:, my_cols], kbuf.at[0, sub], load_sem.at[0]),
        pltpu.make_async_copy(v_hbm.at[:, my_cols], vbuf.at[0, sub], load_sem.at[1]),
        pltpu.make_async_copy(q_hbm.at[:, my_q], q_vm, load_sem.at[2]),
    ]
    for load in loads:
        load.start()

    barrier = pltpu.get_barrier_semaphore()
    pl.semaphore_signal(barrier, inc=1, device_id={"sub": other}, device_id_type=MESH)

    @pl.when(has_prev)
    def _():
        pl.semaphore_signal(barrier, inc=1, device_id={"seq": seq - 1}, device_id_type=MESH)

    @pl.when(has_next)
    def _():
        pl.semaphore_signal(barrier, inc=1, device_id={"seq": seq + 1}, device_id_type=MESH)

    peers = 1 + jnp.minimum(seq, 1) + jnp.minimum(n_seq - 1 - seq, 1)
    pl.semaphore_wait(barrier, peers)

    def remote(src, dst, send, recv, where):
        return pltpu.make_async_remote_copy(
            src_ref=src, dst_ref=dst, send_sem=send, recv_sem=recv, device_id=where, device_id_type=MESH
        )

    def piece_of(piece):
        return pl.ds(piece * piece_rows, piece_rows)

    swaps = [
        remote(
            hbm.at[piece_of(piece), its_cols], buf.at[0, sub, piece_of(piece)],
            swap_sem.at[piece, kind], recv_sem.at[0, sub, piece, kind], {"sub": other},
        )
        for piece in range(pieces)
        for kind, (hbm, buf) in enumerate(((k_hbm, kbuf), (v_hbm, vbuf)))
    ]
    for swap in swaps:
        swap.start()

    def hops(slot, part, piece):
        return [
            remote(
                buf.at[slot, part, piece_of(piece)], buf.at[slot + 1, part, piece_of(piece)],
                hop_sem.at[slot, part, piece, kind], recv_sem.at[slot + 1, part, piece, kind], {"seq": seq + 1},
            )
            for kind, buf in enumerate((kbuf, vbuf))
        ]

    def wait_arrival(slot, part, piece):
        for kind, buf in enumerate((kbuf, vbuf)):
            here = buf.at[slot, part, piece_of(piece)]
            pltpu.make_async_copy(here, here, recv_sem.at[slot, part, piece, kind]).wait()

    def start_hops(slot, part, piece):
        @pl.when(has_next)
        def _():
            for hop in hops(slot, part, piece):
                hop.start()

    loads[0].wait()
    loads[1].wait()
    for piece in range(pieces):
        start_hops(0, sub, piece)

    lane = lax.broadcasted_iota(jnp.int32, (1, LANES), 1)
    lows = jnp.full((1, LANES), 2**30, jnp.int32)
    highs = jnp.full((1, LANES), 2**30, jnp.int32)
    begin = jnp.int32(0)
    for d in range(n_docs):
        end = begin + lengths[d]
        lows = jnp.where(lane == d, begin, lows)
        highs = jnp.where(lane == d, end, highs)
        begin = end
    block = 256

    def fill(i, _):
        row0 = pl.multiple_of(i * block, block)
        base = lax.broadcasted_iota(jnp.int32, (block, LANES), 0) + row0 + seq * rows
        for slot in range(SPAN + 1):
            place = base - slot * rows
            inside = (place >= lows) & (place < highs)
            kx[slot, pl.ds(row0, block), :] = jnp.where(inside, 1.0, 0.0).astype(jnp.bfloat16)
            if slot == 0:
                qx[pl.ds(row0, block), :] = jnp.where(inside, 0.0, BLOCKED).astype(jnp.bfloat16)
        return 0

    lax.fori_loop(0, rows // block, fill, 0)

    for piece in range(pieces):
        wait_arrival(0, other, piece)
        start_hops(0, other, piece)
    loads[2].wait()

    def wide(x, times):
        return jnp.concatenate([x] * times, axis=1)

    def update(slot, part, key0, n_keys, row0, kv, first=False, offset=None, last=False):
        columns = pl.ds(pl.multiple_of(kv * DH, DH), DH)
        if part is None:
            spans = [(p, 0, min(half, n_keys - p * half)) for p in range(2) if n_keys > p * half]
        else:
            spans = [(part, key0, n_keys)]

        def rows_of(buf):
            return [buf[slot, p, pl.ds(k0, n), columns] for p, k0, n in spans]

        docs = [kx[slot, pl.ds(pl.multiple_of(p * half + k0, LANES), n), :] for p, k0, n in spans]
        keys = jnp.concatenate(
            [jnp.concatenate(rows_of(kbuf), axis=0), jnp.concatenate(docs, axis=0)], axis=1)
        vals = jnp.concatenate(
            [jnp.concatenate(rows_of(vbuf), axis=0), jnp.ones((n_keys, DH), jnp.bfloat16)], axis=1)
        q_rows = pl.ds(row0, rows_q)
        if offset is not None:
            row_at = lax.broadcasted_iota(jnp.int32, (rows_q, n_keys), 0) + offset
            causal = lax.broadcasted_iota(jnp.int32, (rows_q, n_keys), 1) <= row_at
        for g in range(group):
            h = kv * group + g
            at_h = pl.ds(pl.multiple_of(h * DH, DH), DH)
            query = jnp.concatenate([q_vm[q_rows, at_h], qx[q_rows, :]], axis=1)
            scores = lax.dot_general(
                query, keys, (((1,), (1,)), ((), ())), preferred_element_type=jnp.float32)
            if offset is not None:
                scores = jnp.where(causal, scores, LEAST)
            peak = jnp.max(scores, axis=1, keepdims=True)
            if first:
                new_top = jnp.broadcast_to(peak, (rows_q, LANES))
            else:
                old_top = top[h, q_rows, :]
                new_top = jnp.maximum(old_top, peak)
            weights = jnp.exp2((scores - wide(new_top, n_keys // LANES)) * SCALE).astype(jnp.bfloat16)
            total = jnp.dot(weights, vals, preferred_element_type=jnp.float32)
            if not first:
                factor = jnp.exp2((old_top - new_top) * SCALE)
                total = acc[h, q_rows, :] * wide(factor, 2) + total
            if last:
                obuf[q_rows, at_h] = (total[:, :DH] / total[:, DH:]).astype(jnp.bfloat16)
            else:
                acc[h, q_rows, :] = total
                top[h, q_rows, :] = new_top

    def sweep(slot, part, key0, n_keys, start, count, first=False, diagonal=False):
        def body(i, _):
            block_at, kv = i // kv_heads, i % kv_heads
            row0 = pl.multiple_of(start + block_at * rows_q, rows_q)
            update(slot, part, key0, n_keys, row0, kv, first, block_at * rows_q if diagonal else None)
            return 0

        lax.fori_loop(0, count * kv_heads, body, 0)

    blocks = rows // rows_q
    n_out = kv_heads * blocks

    def place(i):
        return i // blocks, pl.multiple_of((i % blocks) * rows_q, rows_q)

    def sends(i):
        kv, row0 = place(i)
        width = group * DH
        here = obuf.at[pl.ds(row0, rows_q), pl.ds(pl.multiple_of(kv * width, LANES), width)]
        there = out.at[pl.ds(row0, rows_q), pl.ds(pl.multiple_of(sub * q_cols + kv * width, LANES), width)]
        return (
            remote(here, there, out_send.at[i], out_recv.at[i], {"sub": other}),
            pltpu.make_async_copy(here, there, out_local.at[i]),
        )

    def finish(write):
        def body(i, _):
            write(*place(i))

            @pl.when(i > 0)
            def _():
                for copy in sends(i - 1):
                    copy.start()

            return 0

        lax.fori_loop(0, n_out, body, 0)
        sends(0)[1].wait()
        for copy in sends(n_out - 1):
            copy.start()

    for block_at in range(blocks):
        def own(kv, _):
            row0 = block_at * rows_q
            update(0, None, 0, row0 + rows_q, row0, kv, first=True, offset=row0)
            return 0

        lax.fori_loop(0, kv_heads, own, 0)

    for slot in range(1, SPAN + 1):
        @pl.when(seq >= slot)
        def _():
            for part in (sub, other):
                tail = slot == SPAN and part is other
                for piece in range(pieces):
                    wait_arrival(slot, part, piece)
                    if slot < SPAN:
                        start_hops(slot, part, piece)
                    if tail and piece < pieces - 1:
                        sweep(slot, part, piece * piece_rows, piece_rows, 0, blocks)
                if tail:
                    finish(lambda kv, row0: update(
                        slot, part, half - piece_rows, piece_rows, row0, kv, last=True))
                else:
                    sweep(slot, part, 0, half, 0, blocks)

    @pl.when(seq < SPAN)
    def _():
        def write(kv, row0):
            q_rows = pl.ds(row0, rows_q)
            for g in range(group):
                h = kv * group + g
                total = acc[h, q_rows, :]
                obuf[q_rows, pl.ds(pl.multiple_of(h * DH, DH), DH)] = (
                    total[:, :DH] / total[:, DH:]).astype(jnp.bfloat16)

        finish(write)

    for i in range(n_out):
        far, near = sends(i)
        far.wait()
        if i:
            near.wait()

    for swap in swaps:
        swap.wait_send()

    for slot in range(SPAN):
        @pl.when((seq >= slot) & has_next)
        def _():
            for part in (sub, other):
                for piece in range(pieces):
                    for hop in hops(slot, part, piece):
                        hop.wait_send()


def shards(n_seq, queries, keys, values, doc_lengths):
    rows, q_total = queries.shape
    half, kv_total = keys.shape
    q_cols = q_total // 2
    split_kv = kv_total // DH >= 2
    kv_cols = kv_total // 2 if split_kv else kv_total
    heads = q_cols // DH
    rows_q, pieces = min(512, half), 2
    sizes = (n_seq, rows, half, kv_cols, q_cols, split_kv, doc_lengths.shape[0], rows_q, pieces)
    n_out = kv_cols // DH * (rows // rows_q)
    any_space = pl.BlockSpec(memory_space=pl.ANY)
    dma = pltpu.SemaphoreType.DMA
    return pl.pallas_call(
        functools.partial(attention_kernel, sizes),
        out_shape=jax.ShapeDtypeStruct((rows, q_total), jnp.bfloat16),
        in_specs=[pl.BlockSpec(memory_space=pltpu.SMEM)] + [any_space] * 3,
        out_specs=any_space,
        scratch_shapes=[
            pltpu.VMEM((rows, q_cols), jnp.bfloat16),
            pltpu.VMEM((SPAN + 1, 2, half, kv_cols), jnp.bfloat16),
            pltpu.VMEM((SPAN + 1, 2, half, kv_cols), jnp.bfloat16),
            pltpu.VMEM((rows, LANES), jnp.bfloat16),
            pltpu.VMEM((SPAN + 1, rows, LANES), jnp.bfloat16),
            pltpu.VMEM((heads, rows, LANES), jnp.float32),
            pltpu.VMEM((heads, rows, 2 * DH), jnp.float32),
            pltpu.VMEM((rows, q_cols), jnp.bfloat16),
            dma((3,)),
            dma((pieces, 2)),
            dma((SPAN, 2, pieces, 2)),
            dma((SPAN + 1, 2, pieces, 2)),
            dma((n_out,)),
            dma((n_out,)),
            dma((n_out,)),
        ],
        compiler_params=pltpu.CompilerParams(
            collective_id=0, has_side_effects=True, vmem_limit_bytes=60 * 1024 * 1024
        ),
    )(doc_lengths, queries, keys, values)


def solution(mesh):
    placed = (
        P(("groups", "seq"), "head"),
        P(("groups", "seq", "sub"), "head"),
        P(("groups", "seq", "sub"), "head"),
        P("groups"),
    )
    return jax.shard_map(
        functools.partial(shards, mesh.shape["seq"]),
        mesh=mesh, in_specs=placed, out_specs=P(("groups", "seq"), "head"), check_vma=False,
    )
```

time: 66.6 us -> 63 us (0.946)
  Pallas kernels: 61.6 us -> 58.1 us
    pallas_call x1, Pallas kernels: 61.6 us -> 58.1 us  [shards(): pl.pallas_call(functools.partial(attention_kernel, sizes), out_shape=jax....]
where the time goes in v2:
time: 63 us; the launch traced here: 62.9 us
  Pallas kernels  58.1 us (92%)
  local copies, waits for them, and re-layouts  4.79 us (8%)
    pallas_call x1, Pallas kernels, shards(): pl.pallas_call(functools.partial(attention_kernel, sizes), out_shape=jax....  58.1 us
    unnamed x1, local copies, waits for them, and re-layouts  4.79 us

profile of v2, /device:TPU:17, one launch (start us, length us, event | category | flops | bytes accessed | tf_op | source)
XLA Modules:
  0.0 62.9 jit_solution(10184958105646680590)
XLA Ops:
  0.0 58.1 %shard_map.46 = bf16[1024,2048]{1,0:T(8,128)(2,1)} custom-call(s32[8]{0:T(128)} %lengths.1, bf16[1024,2048]{1,0:T(8,128)(2,1)} %q_hbm.1, bf16[512,512]{1,0:T(8,128)(2,1)} %k_hbm.1, bf16[512,512]{1,0:T(8,128)(2,1)} %v_hbm.1), custom_call_target="tpu_custom_call" | custom-call | tf_op jit(solution)/shard_map/pallas_call | solution.py:287
  58.1 4.8 %copy.6 = bf16[1024,2048]{1,0:T(8,128)(2,1)} copy(bf16[1024,2048]{1,0:T(8,128)(2,1)} %shard_map.46) | data formatting | bytes 8388608
